TPU v7x, 32 devices: a whole 2x2x4 slice. The times are simulated.
32 devices in a mesh: gx: 4 (over y, core), gy: 8 (over z, x).
Axes of the slice: x: 2, y: 2, z: 4, core: 2. Of those that a mesh axis runs over, the one named last changes fastest.
Arguments:
- emission: float32 [512, 8, 128], P(('gx', 'gy')), may hold values from 0.05 to 1
- reflectance: float32 [512, 8, 128], P(('gx', 'gy')), may hold values from 0.5 to 0.98
- form_factors: float32 [8192, 128, 128], P(('gx', 'gy')), as said below
- link_source: int32 [8192], P(('gx', 'gy')), may hold values from 0 to 511, as said below
- link_target: int32 [8192], P(('gx', 'gy')), may hold values from 0 to 511, as said below
- link_length: int32 [8192], P(('gx', 'gy')), may hold values from 32 to 128
- block_count: int32 [32], P(('gx', 'gy')), may hold values from 32 to 256, as said below
Outputs:
- solution: float32 [512, 8, 128], P(('gx', 'gy'))
- residual: float32 [512, 8, 128], P(('gx', 'gy'))
Inputs may be any that keep to these rules, and one draw needn't show every extreme that they name: `form_factors`: entries are nonnegative. `link_source`: block k's source is any cluster; among the blocks held by one device, all blocks whose sources lie on one same device name the same source cluster. `link_target`: block k's target is one of the clusters of the device holding it, clusters (k // 256) * 16 to (k // 256) * 16 + 15. `block_count`: some device has all 256 slots live.
All inputs are finite; a program needn't handle non-finite values.
Results may differ from a plain program's by a relative error of at most 0.0011.
Values sent between devices are 32-bit elements; how exact they have to be, the bound alone decides.
A program may use at most 64 MiB of HBM per device.

v0:
```python
import jax
import jax.numpy as jnp
from jax import lax
from jax.sharding import PartitionSpec as P

ITERS = 3


def local(emission, reflectance, form_factors, link_source, link_target, link_length, block_count):
    clusters = emission.shape[0]
    blocks = form_factors.shape[0]
    patch_count = form_factors.shape[2]
    devices = lax.axis_size(("gx", "gy"))
    group_size = min(16, blocks)
    live_count = block_count[0]
    block_ids = jnp.arange(blocks, dtype=jnp.int32)
    live_block = block_ids < live_count
    owner_dev = link_source // clusters
    local_slot = link_source % clusters
    peer_ids = jnp.arange(devices, dtype=jnp.int32)
    peer_match = (owner_dev[None, :] == peer_ids[:, None]) & live_block[None, :]
    wanted = jnp.max(jnp.where(peer_match, local_slot[None, :], 0), axis=1)
    want_from = lax.all_to_all(wanted, ("gx", "gy"), split_axis=0, concat_axis=0, tiled=True)
    column_ids = jnp.arange(patch_count, dtype=jnp.int32)
    column_mask = ((column_ids[None, :] < link_length[:, None]) & live_block[:, None]).astype(
        jnp.float32
    )
    cluster_ids = jnp.arange(clusters, dtype=jnp.int32)
    target_onehot = (cluster_ids[:, None] == (link_target % clusters)[None, :]).astype(jnp.float32)
    turn_count = (live_count + group_size - 1) // group_size

    def operate(radiance):
        outgoing = radiance[want_from]
        arrived = lax.all_to_all(outgoing, ("gx", "gy"), split_axis=0, concat_axis=0, tiled=True)
        sources = arrived[owner_dev] * column_mask[:, None, :]

        def turn(turn_index, total):
            first_block = turn_index * group_size
            factors = lax.dynamic_slice_in_dim(form_factors, first_block, group_size, 0)
            source_vals = lax.dynamic_slice_in_dim(sources, first_block, group_size, 0)
            onehot_part = lax.dynamic_slice_in_dim(target_onehot, first_block, group_size, 1)
            partial_sum = jnp.einsum(
                "kij,kbj->kbi", factors, source_vals, precision=lax.Precision.HIGHEST
            )
            return total + jnp.dot(
                onehot_part, partial_sum.reshape(group_size, -1), precision=lax.Precision.HIGHEST
            )

        empty_sum = jnp.zeros((clusters, radiance.shape[1] * radiance.shape[2]), jnp.float32)
        gathered = lax.fori_loop(0, turn_count, turn, empty_sum)
        return radiance - reflectance * gathered.reshape(radiance.shape)

    solution = jnp.zeros_like(emission)
    residual = emission
    direction = jnp.zeros_like(emission)
    applied = jnp.zeros_like(emission)
    rho_old = jnp.ones((), jnp.float32)
    alpha_coef = jnp.ones((), jnp.float32)
    omega_coef = jnp.ones((), jnp.float32)
    rho_now = lax.psum(jnp.sum(emission * residual), ("gx", "gy"))
    for iteration in range(ITERS):
        beta_coef = rho_now / rho_old * (alpha_coef / omega_coef)
        direction = residual + beta_coef * (direction - omega_coef * applied)
        applied = operate(direction)
        alpha_coef = rho_now / lax.psum(jnp.sum(emission * applied), ("gx", "gy"))
        middle = residual - alpha_coef * applied
        bounce = operate(middle)
        cross_sum, square_sum, shadow_middle, shadow_bounce = lax.psum(
            (
                jnp.sum(bounce * middle),
                jnp.sum(bounce * bounce),
                jnp.sum(emission * middle),
                jnp.sum(emission * bounce),
            ),
            ("gx", "gy"),
        )
        omega_coef = cross_sum / square_sum
        solution = solution + alpha_coef * direction + omega_coef * middle
        residual = middle - omega_coef * bounce
        rho_old = rho_now
        rho_now = shadow_middle - omega_coef * shadow_bounce
    return (solution, residual)


def solution(mesh):
    in_specs = (
        P(("gx", "gy"), None, None),
        P(("gx", "gy"), None, None),
        P(("gx", "gy"), None, None),
        P(("gx", "gy")),
        P(("gx", "gy")),
        P(("gx", "gy")),
        P(("gx", "gy")),
    )
    out_specs = (P(("gx", "gy"), None, None), P(("gx", "gy"), None, None))
    return jax.shard_map(local, mesh=mesh, in_specs=in_specs, out_specs=out_specs, check_vma=False)
```

profile of v0, /device:TPU:14, one launch (start us, length us, event | category | flops | bytes accessed | tf_op | source)
XLA Modules:
  0.0 708.0 jit_solution(13711820568220223381)
XLA Ops:
  4.4 6.0 all-to-all-start
  10.3 40.6 %psum.98 = f32[]{:T(128)} all-reduce(f32[]{:T(128)} %multiply_reduce_fusion.13), channel_id=1, replica_groups=mesh['gx'=4,'gy'=8] {'gx','gy'}, use_global_device_ids=true, to_apply=%region_1.2 | all-reduce | flops 1 | bytes 8 | tf_op jit(solution)/shard_map/psum | solution.py:60
  55.1 4.8 all-to-all-start.1
  60.8 4.6 all-to-all-done.1
  66.6 16.3 %while.60 = (s32[]{:T(128)}, f32[16,1024]{1,0:T(8,128)S(1)}, s32[]{:T(128)}, f32[16,256]{1,0:T(8,128)S(1)}, f32[256,8,128]{2,1,0:T(8,128)S(1)}, /*index=5*/f32[2...) while((s32[]{:T(128)}, f32[16,1024]{1,0:T(8,128)S(1)}, s32[]{:T(128)}, ...), condition=%wide.region_4.5_spmd, body=%wide.region_3.4_spmd.sunk | while | flops 28327940 | bytes 1385623 | solution.py:50
  66.6 3.0 fusion.99
  69.9 3.0 fusion.99
  79.7 3.0 fusion.99
  84.4 77.1 %psum.99 = f32[]{:T(128)} all-reduce(f32[]{:T(128)} %get-tuple-element.303), channel_id=1, replica_groups=mesh['gx'=4,'gy'=8] {'gx','gy'}, use_global_device_ids=true, to_apply=%region_6.7 | all-reduce | flops 1 | bytes 8 | tf_op jit(solution)/shard_map/psum | solution.py:65
  165.0 4.0 all-to-all-start.2
  169.0 5.5 all-to-all-done.2
  175.6 16.3 %while.61 = (s32[]{:T(128)}, f32[16,1024]{1,0:T(8,128)S(1)}, s32[]{:T(128)}, f32[16,256]{1,0:T(8,128)S(1)}, f32[256,8,128]{2,1,0:T(8,128)S(1)}, /*index=5*/f32[2...) while((s32[]{:T(128)}, f32[16,1024]{1,0:T(8,128)S(1)}, s32[]{:T(128)}, ...), condition=%wide.region_8.9_spmd, body=%wide.region_7.8_spmd.sunk | while | flops 28327940 | bytes 1385623 | solution.py:50
  182.2 3.0 fusion.104
  185.4 3.0 fusion.104
  188.7 3.0 fusion.104
  192.7 77.3 %all-reduce.2 = (f32[]{:T(128)}, f32[]{:T(128)}, f32[]{:T(128)}, f32[]{:T(128)}) all-reduce(f32[]{:T(128)} %get-tuple-element.215, f32[]{:T(128)} %get-tuple-element.214, f32[]{:T(128)} %get-tuple-element.213, f32[]{:T(128)} %get-tuple-element.212), channel_id=1, replica_groups=mesh['gx'=4,'gy'=8] {'gx','gy'}, use_global_device_ids=true, to_apply=%region_14.15 | all-reduce | flops 4 | bytes 32 | tf_op jit(solution)/shard_map/psum | solution.py:68
  277.0 4.0 all-to-all-start.3
  281.1 5.5 all-to-all-done.3
  287.7 16.3 %while.62 = (s32[]{:T(128)}, f32[16,1024]{1,0:T(8,128)S(1)}, s32[]{:T(128)}, f32[16,256]{1,0:T(8,128)S(1)}, f32[256,8,128]{2,1,0:T(8,128)S(1)}, /*index=5*/f32[2...) while((s32[]{:T(128)}, f32[16,1024]{1,0:T(8,128)S(1)}, s32[]{:T(128)}, ...), condition=%wide.region_18.19_spmd, body=%wide.region_17.18_spmd.sunk | while | flops 28327940 | bytes 1385623 | solution.py:50
  304.7 77.1 %psum.104 = f32[]{:T(128)} all-reduce(f32[]{:T(128)} %get-tuple-element.300), channel_id=1, replica_groups=mesh['gx'=4,'gy'=8] {'gx','gy'}, use_global_device_ids=true, to_apply=%region_20.21 | all-reduce | flops 1 | bytes 8 | tf_op jit(solution)/shard_map/psum | solution.py:65
  383.7 4.0 all-to-all-start.4
  387.7 5.5 all-to-all-done.4
  394.3 16.5 %while.63 = (s32[]{:T(128)}, f32[16,1024]{1,0:T(8,128)S(1)}, s32[]{:T(128)}, f32[16,256]{1,0:T(8,128)S(1)}, f32[256,8,128]{2,1,0:T(8,128)S(1)}, /*index=5*/f32[2...) while((s32[]{:T(128)}, f32[16,1024]{1,0:T(8,128)S(1)}, s32[]{:T(128)}, ...), condition=%wide.region_22.23_spmd, body=%wide.region_21.22_spmd.sunk | while | flops 28327940 | bytes 1385623 | solution.py:50
  411.6 77.3 %all-reduce.1 = (f32[]{:T(128)}, f32[]{:T(128)}, f32[]{:T(128)}, f32[]{:T(128)}) all-reduce(f32[]{:T(128)} %get-tuple-element.211, f32[]{:T(128)} %get-tuple-element.210, f32[]{:T(128)} %get-tuple-element.209, f32[]{:T(128)} %get-tuple-element.208), channel_id=1, replica_groups=mesh['gx'=4,'gy'=8] {'gx','gy'}, use_global_device_ids=true, to_apply=%region_28.29 | all-reduce | flops 4 | bytes 32 | tf_op jit(solution)/shard_map/psum | solution.py:68
  494.6 4.0 all-to-all-start.5
  498.6 5.5 all-to-all-done.5
  505.2 16.3 %while.64 = (s32[]{:T(128)}, f32[16,1024]{1,0:T(8,128)S(1)}, s32[]{:T(128)}, f32[16,256]{1,0:T(8,128)S(1)}, f32[256,8,128]{2,1,0:T(8,128)S(1)}, /*index=5*/f32[2...) while((s32[]{:T(128)}, f32[16,1024]{1,0:T(8,128)S(1)}, s32[]{:T(128)}, ...), condition=%wide.region_32.33_spmd, body=%wide.region_31.32_spmd.sunk | while | flops 28327940 | bytes 1385623 | solution.py:50
  522.2 77.1 %psum.109 = f32[]{:T(128)} all-reduce(f32[]{:T(128)} %multiply_reduce_fusion.2), channel_id=1, replica_groups=mesh['gx'=4,'gy'=8] {'gx','gy'}, use_global_device_ids=true, to_apply=%region_34.35 | all-reduce | flops 1 | bytes 8 | tf_op jit(solution)/shard_map/psum | solution.py:65
  601.2 4.0 all-to-all-start.6
  605.3 5.5 all-to-all-done.6
  611.9 16.3 %while.65 = (s32[]{:T(128)}, f32[16,1024]{1,0:T(8,128)S(1)}, s32[]{:T(128)}, f32[16,256]{1,0:T(8,128)S(1)}, f32[256,8,128]{2,1,0:T(8,128)S(1)}, /*index=5*/f32[2...) while((s32[]{:T(128)}, f32[16,1024]{1,0:T(8,128)S(1)}, s32[]{:T(128)}, ...), condition=%wide.region_36.37_spmd, body=%wide.region_35.36_spmd.sunk | while | flops 28327940 | bytes 1385623 | solution.py:50
  628.9 77.1 %all-reduce = (f32[]{:T(128)}, f32[]{:T(128)}) all-reduce(f32[]{:T(128)} %get-tuple-element.207, f32[]{:T(128)} %get-tuple-element.206), channel_id=1, replica_groups=mesh['gx'=4,'gy'=8] {'gx','gy'}, use_global_device_ids=true, to_apply=%region_38.39 | all-reduce | flops 2 | bytes 16 | tf_op jit(solution)/shard_map/psum | solution.py:68
  (114 shorter events, 106.1 us)
Async XLA Ops:
  0.6 191.3 %copy-start = (f32[16,8,128]{2,1,0:T(8,128)S(1)}, f32[16,8,128]{2,1,0:T(8,128)}, u32[]{:S(2)}) copy-start(f32[16,8,128]{2,1,0:T(8,128)} %param.19) | copy-start | bytes 196612
  0.6 191.3 %copy-start.1 = (f32[16,8,128]{2,1,0:T(8,128)S(1)}, f32[16,8,128]{2,1,0:T(8,128)}, u32[]{:S(2)}) copy-start(f32[16,8,128]{2,1,0:T(8,128)} %param.20) | copy-start | bytes 196612
  4.4 48.9 %all-to-all-start = ((s32[32,1,1]{2,1,0:T(1,128)}), s32[32,1,1]{2,1,0:T(1,128)S(1)}, u32[]{:S(2)}, u32[]{:S(2)}) async-start(s32[32,1,1]{2,1,0:T(1,128)} %copy.11), calls=%async_computation | async-start | bytes 32768 | tf_op jit(solution)/shard_map/all_to_all | solution.py:23
  55.1 10.3 %all-to-all-start.1 = ((f32[32,8,128]{2,1,0:T(8,128)}), f32[32,8,128]{2,1,0:T(8,128)S(1)}, u32[]{:S(2)}, u32[]{:S(2)}) async-start(f32[32,8,128]{2,1,0:T(8,128)} %gather_fusion), calls=%async_computation.1 | async-start | bytes 262144 | tf_op jit(solution)/shard_map/all_to_all | solution.py:34
  165.0 9.5 %all-to-all-start.2 = ((f32[32,8,128]{2,1,0:T(8,128)}), f32[32,8,128]{2,1,0:T(8,128)S(1)}, u32[]{:S(2)}, u32[]{:S(2)}) async-start(f32[32,8,128]{2,1,0:T(8,128)} %gather_fusion.2), calls=%async_computation.2 | async-start | bytes 262144 | tf_op jit(solution)/shard_map/all_to_all | solution.py:34
  277.0 9.5 %all-to-all-start.3 = ((f32[32,8,128]{2,1,0:T(8,128)}), f32[32,8,128]{2,1,0:T(8,128)S(1)}, u32[]{:S(2)}, u32[]{:S(2)}) async-start(f32[32,8,128]{2,1,0:T(8,128)} %gather_fusion.4), calls=%async_computation.3 | async-start | bytes 262144 | tf_op jit(solution)/shard_map/all_to_all | solution.py:34
  383.7 9.5 %all-to-all-start.4 = ((f32[32,8,128]{2,1,0:T(8,128)}), f32[32,8,128]{2,1,0:T(8,128)S(1)}, u32[]{:S(2)}, u32[]{:S(2)}) async-start(f32[32,8,128]{2,1,0:T(8,128)} %gather_fusion.6), calls=%async_computation.4 | async-start | bytes 262144 | tf_op jit(solution)/shard_map/all_to_all | solution.py:34
  494.6 9.5 %all-to-all-start.5 = ((f32[32,8,128]{2,1,0:T(8,128)}), f32[32,8,128]{2,1,0:T(8,128)S(1)}, u32[]{:S(2)}, u32[]{:S(2)}) async-start(f32[32,8,128]{2,1,0:T(8,128)} %gather_fusion.8), calls=%async_computation.5 | async-start | bytes 262144 | tf_op jit(solution)/shard_map/all_to_all | solution.py:34
  601.2 9.5 %all-to-all-start.6 = ((f32[32,8,128]{2,1,0:T(8,128)}), f32[32,8,128]{2,1,0:T(8,128)S(1)}, u32[]{:S(2)}, u32[]{:S(2)}) async-start(f32[32,8,128]{2,1,0:T(8,128)} %gather_fusion.10), calls=%async_computation.6 | async-start | bytes 262144 | tf_op jit(solution)/shard_map/all_to_all | solution.py:34
where the time goes:
time: 713 us; the launch traced here: 708 us
  blocking collectives  504 us (71%)
  matrix products  97 us (14%)
  waiting for transfers between devices  31.9 us (4%)
  starting transfers between devices  30.9 us (4%)
  between operations  16.7 us (2%)
  local copies, waits for them, and re-layouts  14.3 us (2%)
  other arithmetic  12.4 us (2%)
    psum x3, blocking collectives, local(): lax.psum((jnp.sum(bounce * middle), jnp.sum(bounce * bounce), jnp.sum(emi...  232 us
    psum x3, blocking collectives, local(): alpha_coef = rho_now / lax.psum(jnp.sum(emission * applied), ('gx', 'gy'))  231 us
    dot_general x30, matrix products, turn(): jnp.einsum('kij,kbj->kbi', factors, source_vals, precision=lax.Precision....  88.6 us
    psum x1, blocking collectives, local(): rho_now = lax.psum(jnp.sum(emission * residual), ('gx', 'gy'))  40.6 us
    all_to_all x6, waiting for transfers between devices, operate(): lax.all_to_all(outgoing, ('gx', 'gy'), split_axis=0, concat_axis=0, tiled...  31.9 us
    all_to_all x6, starting transfers between devices, operate(): lax.all_to_all(outgoing, ('gx', 'gy'), split_axis=0, concat_axis=0, tiled...  24.9 us
  transfers between devices with their start and end apart: 7, of which 6 were waited for; matrix products, arithmetic and copies ran while one was open for 0% of the time, Pallas kernels for 0%

commit v1 on v0

--- a/solution.py
+++ b/solution.py
@@ -65,14 +65,19 @@
         alpha_coef = rho_now / lax.psum(jnp.sum(emission * applied), ("gx", "gy"))
         middle = residual - alpha_coef * applied
         bounce = operate(middle)
-        cross_sum, square_sum, shadow_middle, shadow_bounce = lax.psum(
+
+        def draft_rings(obj):
+            kept_arr = lax.psum(obj, axis_name="gy")
+            inter = lax.psum(kept_arr, axis_name="gx")
+            return inter
+
+        cross_sum, square_sum, shadow_middle, shadow_bounce = draft_rings(
             (
                 jnp.sum(bounce * middle),
                 jnp.sum(bounce * bounce),
                 jnp.sum(emission * middle),
                 jnp.sum(emission * bounce),
-            ),
-            ("gx", "gy"),
+            )
         )
         omega_coef = cross_sum / square_sum
         solution = solution + alpha_coef * direction + omega_coef * middle

time: 713 us -> 671 us (0.941)
  the two profiles are of different devices: /device:TPU:14 before, /device:TPU:0 now
where the time goes in v1:
time: 671 us; the launch traced here: 666 us
  blocking collectives  481 us (72%)
  matrix products  58.2 us (9%)
  waiting for transfers between devices  46 us (7%)
  starting transfers between devices  36.3 us (5%)
  between operations  16.7 us (2%)
  local copies, waits for them, and re-layouts  14.3 us (2%)
  other arithmetic  12.5 us (2%)
    psum x3, blocking collectives, local(): alpha_coef = rho_now / lax.psum(jnp.sum(emission * applied), ('gx', 'gy'))  237 us
    psum x3, blocking collectives, draft_rings(): kept_arr = lax.psum(obj, axis_name='gy')  184 us
    dot_general x18, matrix products, turn(): jnp.einsum('kij,kbj->kbi', factors, source_vals, precision=lax.Precision....  53.1 us
    all_to_all x6, waiting for transfers between devices, operate(): lax.all_to_all(outgoing, ('gx', 'gy'), split_axis=0, concat_axis=0, tiled...  46 us
    psum x1, blocking collectives, local(): rho_now = lax.psum(jnp.sum(emission * residual), ('gx', 'gy'))  40.7 us
    all_to_all x6, starting transfers between devices, operate(): lax.all_to_all(outgoing, ('gx', 'gy'), split_axis=0, concat_axis=0, tiled...  29 us
    psum x3, blocking collectives, draft_rings(): inter = lax.psum(kept_arr, axis_name='gx')  19.3 us
  transfers between devices with their start and end apart: 7, of which 6 were waited for; matrix products, arithmetic and copies ran while one was open for 0% of the time, Pallas kernels for 0%

profile of v1, /device:TPU:0, one launch (start us, length us, event | category | flops | bytes accessed | tf_op | source)
XLA Modules:
  0.0 665.7 jit_solution(17408464863754330313)
XLA Ops:
  4.4 7.3 %all-to-all-start = ((s32[32,1,1]{2,1,0:T(1,128)}), s32[32,1,1]{2,1,0:T(1,128)S(1)}, u32[]{:S(2)}, u32[]{:S(2)}) async-start(s32[32,1,1]{2,1,0:T(1,128)} %copy.11), calls=%async_computation | async-start | bytes 32768 | tf_op jit(solution)/shard_map/all_to_all | solution.py:23
  11.7 40.7 %psum.168 = f32[]{:T(128)} all-reduce(f32[]{:T(128)} %multiply_reduce_fusion.13), channel_id=1, replica_groups=mesh['gx'=4,'gy'=8] {'gx','gy'}, use_global_device_ids=true, to_apply=%region_1.2 | all-reduce | flops 1 | bytes 8 | tf_op jit(solution)/shard_map/psum | solution.py:60
  56.6 4.7 all-to-all-start.1
  62.2 7.0 %all-to-all-done.1 = f32[32,8,128]{2,1,0:T(8,128)S(1)} async-done(((f32[32,8,128]{2,1,0:T(8,128)}), f32[32,8,128]{2,1,0:T(8,128)S(1)}, u32[]{:S(2)}, u32[]{:S(2)}) %all-to-all-start.1) | async-done | bytes 131104 | tf_op jit(solution)/shard_map/all_to_all | solution.py:34
  70.3 9.8 %while.60 = (s32[]{:T(128)}, f32[16,1024]{1,0:T(8,128)S(1)}, s32[]{:T(128)}, f32[16,256]{1,0:T(8,128)S(1)}, f32[256,8,128]{2,1,0:T(8,128)S(1)}, /*index=5*/f32[2...) while((s32[]{:T(128)}, f32[16,1024]{1,0:T(8,128)S(1)}, s32[]{:T(128)}, ...), condition=%wide.region_4.5_spmd, body=%wide.region_3.4_spmd.sunk | while | flops 28327940 | bytes 1385623 | solution.py:50
  70.3 3.0 fusion.99
  73.6 3.0 fusion.99
  81.6 78.9 %psum.169 = f32[]{:T(128)} all-reduce(f32[]{:T(128)} %get-tuple-element.313), channel_id=1, replica_groups=mesh['gx'=4,'gy'=8] {'gx','gy'}, use_global_device_ids=true, to_apply=%region_6.7 | all-reduce | flops 1 | bytes 8 | tf_op jit(solution)/shard_map/psum | solution.py:65
  164.0 6.4 all-to-all-start.2
  170.4 7.8 %all-to-all-done.2 = f32[32,8,128]{2,1,0:T(8,128)S(1)} async-done(((f32[32,8,128]{2,1,0:T(8,128)}), f32[32,8,128]{2,1,0:T(8,128)S(1)}, u32[]{:S(2)}, u32[]{:S(2)}) %all-to-all-start.2) | async-done | bytes 131104 | tf_op jit(solution)/shard_map/all_to_all | solution.py:34
  179.3 9.8 %while.61 = (s32[]{:T(128)}, f32[16,1024]{1,0:T(8,128)S(1)}, s32[]{:T(128)}, f32[16,256]{1,0:T(8,128)S(1)}, f32[256,8,128]{2,1,0:T(8,128)S(1)}, /*index=5*/f32[2...) while((s32[]{:T(128)}, f32[16,1024]{1,0:T(8,128)S(1)}, s32[]{:T(128)}, ...), condition=%wide.region_8.9_spmd, body=%wide.region_7.8_spmd.sunk | while | flops 28327940 | bytes 1385623 | solution.py:50
  189.9 61.4 %all-reduce.2 = (f32[]{:T(128)}, f32[]{:T(128)}, f32[]{:T(128)}, f32[]{:T(128)}) all-reduce(f32[]{:T(128)} %get-tuple-element.215, f32[]{:T(128)} %get-tuple-element.214, f32[]{:T(128)} %get-tuple-element.213, f32[]{:T(128)} %get-tuple-element.212), channel_id=1, replica_groups=mesh['gx'=4,'gy'=8] {'gy'}, use_global_device_ids=true, to_apply=%region_16.17 | all-reduce | flops 4 | bytes 32 | tf_op jit(solution)/shard_map/psum | solution.py:70
  251.3 6.5 all-reduce.5
  267.4 7.8 %all-to-all-done.3 = f32[32,8,128]{2,1,0:T(8,128)S(1)} async-done(((f32[32,8,128]{2,1,0:T(8,128)}), f32[32,8,128]{2,1,0:T(8,128)S(1)}, u32[]{:S(2)}, u32[]{:S(2)}) %all-to-all-start.3) | async-done | bytes 131104 | tf_op jit(solution)/shard_map/all_to_all | solution.py:34
  276.4 9.8 %while.62 = (s32[]{:T(128)}, f32[16,1024]{1,0:T(8,128)S(1)}, s32[]{:T(128)}, f32[16,256]{1,0:T(8,128)S(1)}, f32[256,8,128]{2,1,0:T(8,128)S(1)}, /*index=5*/f32[2...) while((s32[]{:T(128)}, f32[16,1024]{1,0:T(8,128)S(1)}, s32[]{:T(128)}, ...), condition=%wide.region_22.23_spmd, body=%wide.region_21.22_spmd.sunk | while | flops 28327940 | bytes 1385623 | solution.py:50
  286.8 78.9 %psum.178 = f32[]{:T(128)} all-reduce(f32[]{:T(128)} %get-tuple-element.310), channel_id=1, replica_groups=mesh['gx'=4,'gy'=8] {'gx','gy'}, use_global_device_ids=true, to_apply=%region_24.25 | all-reduce | flops 1 | bytes 8 | tf_op jit(solution)/shard_map/psum | solution.py:65
  367.7 6.4 all-to-all-start.4
  374.0 7.8 %all-to-all-done.4 = f32[32,8,128]{2,1,0:T(8,128)S(1)} async-done(((f32[32,8,128]{2,1,0:T(8,128)}), f32[32,8,128]{2,1,0:T(8,128)S(1)}, u32[]{:S(2)}, u32[]{:S(2)}) %all-to-all-start.4) | async-done | bytes 131104 | tf_op jit(solution)/shard_map/all_to_all | solution.py:34
  383.0 10.0 %while.63 = (s32[]{:T(128)}, f32[16,1024]{1,0:T(8,128)S(1)}, s32[]{:T(128)}, f32[16,256]{1,0:T(8,128)S(1)}, f32[256,8,128]{2,1,0:T(8,128)S(1)}, /*index=5*/f32[2...) while((s32[]{:T(128)}, f32[16,1024]{1,0:T(8,128)S(1)}, s32[]{:T(128)}, ...), condition=%wide.region_26.27_spmd, body=%wide.region_25.26_spmd.sunk | while | flops 28327940 | bytes 1385623 | solution.py:50
  383.2 3.0 fusion.114
  389.8 3.0 fusion.114
  393.8 61.4 %all-reduce.1 = (f32[]{:T(128)}, f32[]{:T(128)}, f32[]{:T(128)}, f32[]{:T(128)}) all-reduce(f32[]{:T(128)} %get-tuple-element.211, f32[]{:T(128)} %get-tuple-element.210, f32[]{:T(128)} %get-tuple-element.209, f32[]{:T(128)} %get-tuple-element.208), channel_id=1, replica_groups=mesh['gx'=4,'gy'=8] {'gy'}, use_global_device_ids=true, to_apply=%region_34.35 | all-reduce | flops 4 | bytes 32 | tf_op jit(solution)/shard_map/psum | solution.py:70
  455.2 6.5 all-reduce.4
  469.9 7.8 %all-to-all-done.5 = f32[32,8,128]{2,1,0:T(8,128)S(1)} async-done(((f32[32,8,128]{2,1,0:T(8,128)}), f32[32,8,128]{2,1,0:T(8,128)S(1)}, u32[]{:S(2)}, u32[]{:S(2)}) %all-to-all-start.5) | async-done | bytes 131104 | tf_op jit(solution)/shard_map/all_to_all | solution.py:34
  478.8 9.8 %while.64 = (s32[]{:T(128)}, f32[16,1024]{1,0:T(8,128)S(1)}, s32[]{:T(128)}, f32[16,256]{1,0:T(8,128)S(1)}, f32[256,8,128]{2,1,0:T(8,128)S(1)}, /*index=5*/f32[2...) while((s32[]{:T(128)}, f32[16,1024]{1,0:T(8,128)S(1)}, s32[]{:T(128)}, ...), condition=%wide.region_40.41_spmd, body=%wide.region_39.40_spmd.sunk | while | flops 28327940 | bytes 1385623 | solution.py:50
  478.9 3.0 fusion.119
  489.3 78.9 %psum.187 = f32[]{:T(128)} all-reduce(f32[]{:T(128)} %multiply_reduce_fusion.2), channel_id=1, replica_groups=mesh['gx'=4,'gy'=8] {'gx','gy'}, use_global_device_ids=true, to_apply=%region_42.43 | all-reduce | flops 1 | bytes 8 | tf_op jit(solution)/shard_map/psum | solution.py:65
  570.1 6.4 all-to-all-start.6
  576.5 7.8 %all-to-all-done.6 = f32[32,8,128]{2,1,0:T(8,128)S(1)} async-done(((f32[32,8,128]{2,1,0:T(8,128)}), f32[32,8,128]{2,1,0:T(8,128)S(1)}, u32[]{:S(2)}, u32[]{:S(2)}) %all-to-all-start.6) | async-done | bytes 131104 | tf_op jit(solution)/shard_map/all_to_all | solution.py:34
  585.5 9.8 %while.65 = (s32[]{:T(128)}, f32[16,1024]{1,0:T(8,128)S(1)}, s32[]{:T(128)}, f32[16,256]{1,0:T(8,128)S(1)}, f32[256,8,128]{2,1,0:T(8,128)S(1)}, /*index=5*/f32[2...) while((s32[]{:T(128)}, f32[16,1024]{1,0:T(8,128)S(1)}, s32[]{:T(128)}, ...), condition=%wide.region_44.45_spmd, body=%wide.region_43.44_spmd.sunk | while | flops 28327940 | bytes 1385623 | solution.py:50
  596.0 61.3 %all-reduce = (f32[]{:T(128)}, f32[]{:T(128)}) all-reduce(f32[]{:T(128)} %get-tuple-element.207, f32[]{:T(128)} %get-tuple-element.206), channel_id=1, replica_groups=mesh['gx'=4,'gy'=8] {'gy'}, use_global_device_ids=true, to_apply=%region_46.47 | all-reduce | flops 2 | bytes 16 | tf_op jit(solution)/shard_map/psum | solution.py:70
  657.3 6.4 all-reduce.3
  (93 shorter events, 75.4 us)
Async XLA Ops:
  0.6 188.5 %copy-start = (f32[16,8,128]{2,1,0:T(8,128)S(1)}, f32[16,8,128]{2,1,0:T(8,128)}, u32[]{:S(2)}) copy-start(f32[16,8,128]{2,1,0:T(8,128)} %param.19) | copy-start | bytes 196612
  0.6 188.5 %copy-start.1 = (f32[16,8,128]{2,1,0:T(8,128)S(1)}, f32[16,8,128]{2,1,0:T(8,128)}, u32[]{:S(2)}) copy-start(f32[16,8,128]{2,1,0:T(8,128)} %param.20) | copy-start | bytes 196612
  4.4 50.3 %all-to-all-start = ((s32[32,1,1]{2,1,0:T(1,128)}), s32[32,1,1]{2,1,0:T(1,128)S(1)}, u32[]{:S(2)}, u32[]{:S(2)}) async-start(s32[32,1,1]{2,1,0:T(1,128)} %copy.11), calls=%async_computation | async-start | bytes 32768 | tf_op jit(solution)/shard_map/all_to_all | solution.py:23
  56.6 12.6 %all-to-all-start.1 = ((f32[32,8,128]{2,1,0:T(8,128)}), f32[32,8,128]{2,1,0:T(8,128)S(1)}, u32[]{:S(2)}, u32[]{:S(2)}) async-start(f32[32,8,128]{2,1,0:T(8,128)} %gather_fusion), calls=%async_computation.1 | async-start | bytes 262144 | tf_op jit(solution)/shard_map/all_to_all | solution.py:34
  164.0 14.2 %all-to-all-start.2 = ((f32[32,8,128]{2,1,0:T(8,128)}), f32[32,8,128]{2,1,0:T(8,128)S(1)}, u32[]{:S(2)}, u32[]{:S(2)}) async-start(f32[32,8,128]{2,1,0:T(8,128)} %gather_fusion.2), calls=%async_computation.2 | async-start | bytes 262144 | tf_op jit(solution)/shard_map/all_to_all | solution.py:34
  264.8 10.4 %all-to-all-start.3 = ((f32[32,8,128]{2,1,0:T(8,128)}), f32[32,8,128]{2,1,0:T(8,128)S(1)}, u32[]{:S(2)}, u32[]{:S(2)}) async-start(f32[32,8,128]{2,1,0:T(8,128)} %gather_fusion.4), calls=%async_computation.3 | async-start | bytes 262144 | tf_op jit(solution)/shard_map/all_to_all | solution.py:34
  367.7 14.2 %all-to-all-start.4 = ((f32[32,8,128]{2,1,0:T(8,128)}), f32[32,8,128]{2,1,0:T(8,128)S(1)}, u32[]{:S(2)}, u32[]{:S(2)}) async-start(f32[32,8,128]{2,1,0:T(8,128)} %gather_fusion.6), calls=%async_computation.4 | async-start | bytes 262144 | tf_op jit(solution)/shard_map/all_to_all | solution.py:34
  467.3 10.4 %all-to-all-start.5 = ((f32[32,8,128]{2,1,0:T(8,128)}), f32[32,8,128]{2,1,0:T(8,128)S(1)}, u32[]{:S(2)}, u32[]{:S(2)}) async-start(f32[32,8,128]{2,1,0:T(8,128)} %gather_fusion.8), calls=%async_computation.5 | async-start | bytes 262144 | tf_op jit(solution)/shard_map/all_to_all | solution.py:34
  570.1 14.2 %all-to-all-start.6 = ((f32[32,8,128]{2,1,0:T(8,128)}), f32[32,8,128]{2,1,0:T(8,128)S(1)}, u32[]{:S(2)}, u32[]{:S(2)}) async-start(f32[32,8,128]{2,1,0:T(8,128)} %gather_fusion.10), calls=%async_computation.6 | async-start | bytes 262144 | tf_op jit(solution)/shard_map/all_to_all | solution.py:34
